TPU v7x, 8 devices: a whole 2x2x1 slice. The times are simulated.
8 devices in a mesh: rep: 1 (over z), dp: 8 (over x, y, core).
Axes of the slice: x: 2, y: 2, z: 1, core: 2. Of those that a mesh axis runs over, the one named last changes fastest.
Arguments:
- g_w_gate: bfloat16 [8, 2, 1024, 3328], P(('rep', 'dp'))
- g_w_up: bfloat16 [8, 2, 1024, 3328], P(('rep', 'dp'))
- g_w_down: bfloat16 [8, 2, 3328, 1024], P(('rep', 'dp'))
- w_gate: bfloat16 [2, 1024, 3328], replicated
- w_up: bfloat16 [2, 1024, 3328], replicated
- w_down: bfloat16 [2, 3328, 1024], replicated
- m_w_gate: float32 [2, 1024, 3328], P(None, 'dp')
- m_w_up: float32 [2, 1024, 3328], P(None, 'dp')
- m_w_down: float32 [2, 3328, 1024], P(None, 'dp')
- v_w_gate: float32 [2, 1024, 3328], P(None, 'dp')
- v_w_up: float32 [2, 1024, 3328], P(None, 'dp')
- v_w_down: float32 [2, 3328, 1024], P(None, 'dp')
Outputs:
- output 1: bfloat16 [2, 1024, 3328], P('rep')
- output 2: bfloat16 [2, 1024, 3328], P('rep')
- output 3: bfloat16 [2, 3328, 1024], P('rep')
- output 4: float32 [2, 1024, 3328], P('rep', 'dp')
- output 5: float32 [2, 1024, 3328], P('rep', 'dp')
- output 6: float32 [2, 3328, 1024], P('rep', 'dp')
- output 7: float32 [2, 1024, 3328], P('rep', 'dp')
- output 8: float32 [2, 1024, 3328], P('rep', 'dp')
- output 9: float32 [2, 3328, 1024], P('rep', 'dp')
All inputs are finite; a program needn't handle non-finite values.
Results may differ from a plain program's by a relative error of at most 0.022.
Values are sent between devices in bfloat16 or wider.
A program may use at most 2 GiB of HBM per device.

v0:
```python
import jax
import jax.numpy as jnp
from jax import lax
from jax.sharding import PartitionSpec as P


def adamw(w, m, v, g):
    m = 0.9 * m + 0.1 * g
    v = 0.95 * v + 0.05 * g * g
    step = m * lax.rsqrt(v + 1e-8) + 0.1 * w
    return (w - 0.02 * step).astype(jnp.bfloat16), m, v


def clipped(gradients, sum_of_squares, count):
    factor = jnp.minimum(1.0, 0.5 * lax.rsqrt(sum_of_squares / count + 1e-30))
    return [g * factor for g in gradients]


def solution(mesh):
    def step(*arrays):
        terms, weights, m, v = (arrays[i : i + 3] for i in (0, 3, 6, 9))
        gradients = [lax.psum_scatter(t[0], "dp", scatter_dimension=1, tiled=True).astype(jnp.float32) for t in terms]
        squares = lax.psum(sum(jnp.sum(g * g) for g in gradients), "dp")
        gradients = clipped(gradients, squares, lax.psum(1, "dp") * sum(g.size for g in gradients))
        me = lax.axis_index("dp")
        own = [lax.dynamic_slice_in_dim(w, me * one.shape[1], one.shape[1], 1).astype(jnp.float32) for w, one in zip(weights, m, strict=True)]
        new = [adamw(w, m, v, g) for w, m, v, g in zip(own, m, v, gradients, strict=True)]
        whole = [lax.all_gather(one[0], "dp", axis=1, tiled=True) for one in new]
        return (*whole, *(one[1] for one in new), *(one[2] for one in new))

    all_of, cut = P(None, None, None), P(None, "dp", None)
    return jax.shard_map(
        step,
        mesh=mesh,
        in_specs=(P(("rep", "dp"), None, None, None),) * 3 + (all_of,) * 3 + (cut,) * 6,
        out_specs=(P("rep", None, None),) * 3 + (P("rep", "dp", None),) * 6,
        check_vma=False,
    )
```

profile of v0, /device:TPU:0, one launch (start us, length us, event | category | flops | bytes accessed | tf_op | source)
XLA Modules:
  0.0 574.5 jit_solution(6767704665347427387)
XLA Ops:
  7.2 0.0 reduce-scatter.4.cloned.1.call-start
  7.2 0.7 reduce-scatter.4.cloned.1.call-update
  7.9 0.0 reduce-scatter.6.cloned.1.call-start
  8.0 0.7 reduce-scatter.6.cloned.1.call-update
  8.7 0.0 reduce-scatter.8.cloned.1.call-start
  8.7 0.7 reduce-scatter.8.cloned.1.call-update
  9.4 0.0 all-gather.8.cloned.1.call-start
  9.4 93.7 %reduce-scatter.4.cloned.1.call-done = bf16[2,128,3328]{2,1,0:T(8,128)(2,1)} async-done(((bf16[2,1024,3328]{2,1,0:T(8,128)(2,1)}), bf16[2,128,3328]{2,1,0:T(8,128)(2,1)}) %reduce-scatter.4.cloned.1.call-update) | async-done | bytes 1703952 | tf_op jit(solution)/shard_map/reduce_scatter | solution.py:22
  103.1 2.9 fusion.9
  106.1 89.4 %reduce-scatter.6.cloned.1.call-done = bf16[2,128,3328]{2,1,0:T(8,128)(2,1)} async-done(((bf16[2,1024,3328]{2,1,0:T(8,128)(2,1)}), bf16[2,128,3328]{2,1,0:T(8,128)(2,1)}) %reduce-scatter.6.cloned.1.call-update) | async-done | bytes 1703952 | tf_op jit(solution)/shard_map/reduce_scatter | solution.py:22
  195.5 2.9 fusion.10
  199.7 88.1 %reduce-scatter.8.cloned.1.call-done = bf16[2,416,1024]{2,1,0:T(8,128)(2,1)} async-done(((bf16[2,3328,1024]{2,1,0:T(8,128)(2,1)}), bf16[2,416,1024]{2,1,0:T(8,128)(2,1)}) %reduce-scatter.8.cloned.1.call-update) | async-done | bytes 1703952 | tf_op jit(solution)/shard_map/reduce_scatter | solution.py:22
  287.9 2.9 fusion.11
  291.5 22.2 %psum.7 = f32[]{:T(128)} all-reduce(f32[]{:T(128)S(6)} %add.65), channel_id=1, replica_groups=mesh['rep'=1,'dp'=8] {'dp'}, use_global_device_ids=true, to_apply=%region_6.0 | all-reduce | flops 1 | bytes 8 | tf_op jit(solution)/shard_map/psum | solution.py:23
  314.4 0.0 copy-start.2
  314.4 6.7 %fusion.17 = (bf16[2,416,1024]{2,1,0:T(8,128)(2,1)}, f32[2,416,1024]{2,1,0:T(8,128)}, f32[2,416,1024]{2,1,0:T(8,128)}) fusion(bf16[2,3328,1024]{2,1,0:T(8,128)(2,1)} %param.17, s32[]{:T(128)S(6)} %select_n.8, f32[]{:T(128)S(6)} %min_shard_map.3, bf16[2,416,1024]{2,1,0:T(8,128)(2,1)} %reduce-scatter.8.cloned.1.call-done, f32[2,416,1024]{2,1,0:T(8,128)} %param.23, ...), kind=kLoop, calls=%fused_computation.32 | loop fusion | flops 14483456 | bytes 18743304 | tf_op jit(solution)/shard_map/convert_element_type | solution.py:11
  321.1 0.0 all-gather.8.cloned.1.call-update
  321.1 0.0 all-gather.4.cloned.1.call-start
  321.2 0.0 copy-done.2
  321.2 0.0 copy-start.1
  321.2 6.4 %fusion.8 = (bf16[2,128,3328]{2,1,0:T(8,128)(2,1)}, f32[2,128,3328]{2,1,0:T(8,128)}, f32[2,128,3328]{2,1,0:T(8,128)}) fusion(bf16[2,1024,3328]{2,1,0:T(8,128)(2,1)} %param.15, s32[]{:T(128)S(6)} %select_n.7, f32[]{:T(128)S(6)} %min_shard_map.3, bf16[2,128,3328]{2,1,0:T(8,128)(2,1)S(1)} %copy-done.2, f32[2,128,3328]{2,1,0:T(8,128)} %param.21, ...), kind=kLoop, calls=%fused_computation.23 | loop fusion | flops 14483456 | bytes 18743304 | tf_op jit(solution)/shard_map/convert_element_type | solution.py:11
  327.6 0.0 all-gather.4.cloned.1.call-update
  327.6 0.0 all-gather.6.cloned.1.call-start
  327.6 0.0 copy-done.1
  327.7 7.9 %fusion.14 = (bf16[2,128,3328]{2,1,0:T(8,128)(2,1)}, f32[2,128,3328]{2,1,0:T(8,128)}, f32[2,128,3328]{2,1,0:T(8,128)}) fusion(bf16[2,1024,3328]{2,1,0:T(8,128)(2,1)} %param.16, s32[]{:T(128)S(6)} %select_n.7, f32[]{:T(128)S(6)} %min_shard_map.3, bf16[2,128,3328]{2,1,0:T(8,128)(2,1)S(1)} %copy-done.1, f32[2,128,3328]{2,1,0:T(8,128)} %param.22, ...), kind=kLoop, calls=%fused_computation.29 | loop fusion | flops 14483456 | bytes 18743304 | tf_op jit(solution)/shard_map/convert_element_type | solution.py:11
  335.5 0.0 all-gather.6.cloned.1.call-update
  335.5 58.5 %all-gather.8.cloned.1.call-done = bf16[2,3328,1024]{2,1,0:T(8,128)(2,1)} async-done(((bf16[2,416,1024]{2,1,0:T(8,128)(2,1)}), bf16[2,3328,1024]{2,1,0:T(8,128)(2,1)}) %all-gather.8.cloned.1.call-update) | async-done | bytes 13631504 | tf_op jit(solution)/shard_map/all_gather | solution.py:28
  394.1 73.2 %all-gather.4.cloned.1.call-done = bf16[2,1024,3328]{2,1,0:T(8,128)(2,1)} async-done(((bf16[2,128,3328]{2,1,0:T(8,128)(2,1)}), bf16[2,1024,3328]{2,1,0:T(8,128)(2,1)}) %all-gather.4.cloned.1.call-update) | async-done | bytes 13631504 | tf_op jit(solution)/shard_map/all_gather | solution.py:28
  467.2 73.2 %all-gather.6.cloned.1.call-done = bf16[2,1024,3328]{2,1,0:T(8,128)(2,1)} async-done(((bf16[2,128,3328]{2,1,0:T(8,128)(2,1)}), bf16[2,1024,3328]{2,1,0:T(8,128)(2,1)}) %all-gather.6.cloned.1.call-update) | async-done | bytes 13631504 | tf_op jit(solution)/shard_map/all_gather | solution.py:28
  540.4 0.0 copy-start
  540.4 0.0 slice-start
  540.4 0.0 slice-start.1
  540.4 15.1 %copy.24 = bf16[2,1024,3328]{2,1,0:T(8,128)(2,1)} copy(bf16[2,1024,3328]{2,1,0:T(8,128)(2,1)} %all-gather.4.cloned.1.call-done) | data formatting | bytes 27262976
  555.4 0.0 copy-done
  555.4 0.0 slice-start.2
  555.5 0.0 slice-start.3
  555.5 6.6 %copy.25 = bf16[2,1024,3328]{2,1,0:T(8,128)(2,1)} copy(bf16[2,1024,3328]{2,1,0:T(8,128)(2,1)S(1)} %copy-done) | data formatting | bytes 27262976
  562.0 0.0 slice-done
  562.0 0.0 slice-done.1
  562.0 0.0 slice-done.2
  562.0 0.5 slice-done.3
  562.5 5.1 copy.26
  (1 shorter events, 0.0 us)
Async XLA Ops:
  7.2 96.0 %reduce-scatter.4.cloned.1.call-start = ((), (), s32[]{:S(2)}) async-start(), calls=%async_computation.3 | async-start | bytes 15335424 | tf_op jit(solution)/shard_map/reduce_scatter | solution.py:22
  7.9 187.6 %reduce-scatter.6.cloned.1.call-start = ((), (), s32[]{:S(2)}) async-start(), calls=%async_computation.4 | async-start | bytes 15335424 | tf_op jit(solution)/shard_map/reduce_scatter | solution.py:22
  8.7 279.2 %reduce-scatter.8.cloned.1.call-start = ((), (), s32[]{:S(2)}) async-start(), calls=%async_computation.5 | async-start | bytes 15335424 | tf_op jit(solution)/shard_map/reduce_scatter | solution.py:22
  9.4 384.7 %all-gather.8.cloned.1.call-start = ((), (), s32[]{:S(2)}) async-start(), calls=%async_computation.8 | async-start | bytes 15335424 | tf_op jit(solution)/shard_map/all_gather | solution.py:28
  314.4 6.8 %copy-start.2 = (bf16[2,128,3328]{2,1,0:T(8,128)(2,1)S(1)}, bf16[2,128,3328]{2,1,0:T(8,128)(2,1)}, u32[]{:S(2)}) copy-start(bf16[2,128,3328]{2,1,0:T(8,128)(2,1)} %reduce-scatter.4.cloned.1.call-done) | copy-start | bytes 5111812
  321.1 146.1 %all-gather.4.cloned.1.call-start = ((), (), s32[]{:S(2)}) async-start(), calls=%async_computation.6 | async-start | bytes 15335424 | tf_op jit(solution)/shard_map/all_gather | solution.py:28
  321.2 6.5 %copy-start.1 = (bf16[2,128,3328]{2,1,0:T(8,128)(2,1)S(1)}, bf16[2,128,3328]{2,1,0:T(8,128)(2,1)}, u32[]{:S(2)}) copy-start(bf16[2,128,3328]{2,1,0:T(8,128)(2,1)} %reduce-scatter.6.cloned.1.call-done) | copy-start | bytes 5111812
  327.6 212.8 %all-gather.6.cloned.1.call-start = ((), (), s32[]{:S(2)}) async-start(), calls=%async_computation.7 | async-start | bytes 15335424 | tf_op jit(solution)/shard_map/all_gather | solution.py:28
  540.4 15.1 %copy-start = (bf16[2,1024,3328]{2,1,0:T(8,128)(2,1)S(1)}, bf16[2,1024,3328]{2,1,0:T(8,128)(2,1)}, u32[]{:S(2)}) copy-start(bf16[2,1024,3328]{2,1,0:T(8,128)(2,1)} %all-gather.6.cloned.1.call-done) | copy-start | bytes 40894468
  540.4 21.6 %slice-start = ((s8[13631488]{0:T(1024)(128)(4,1)}), s8[4194304]{0:T(1024)(128)(4,1)S(1)}, s32[]{:S(2)}) async-start(s8[13631488]{0:T(1024)(128)(4,1)} %bitcast.6), calls=%async_computation.9 | async-start | bytes 8388608
  540.4 21.6 %slice-start.1 = ((s8[13631488]{0:T(1024)(128)(4,1)}), s8[4194304]{0:T(1024)(128)(4,1)S(1)}, s32[]{:S(2)}) async-start(s8[13631488]{0:T(1024)(128)(4,1)} %bitcast.6), calls=%async_computation.10 | async-start | bytes 8388608
  555.4 6.6 %slice-start.2 = ((s8[13631488]{0:T(1024)(128)(4,1)}), s8[4194304]{0:T(1024)(128)(4,1)S(1)}, s32[]{:S(2)}) async-start(s8[13631488]{0:T(1024)(128)(4,1)} %bitcast.6), calls=%async_computation.11 | async-start | bytes 8388608
  555.5 7.1 %slice-start.3 = ((s8[13631488]{0:T(1024)(128)(4,1)}), s8[1048576]{0:T(1024)(128)(4,1)S(1)}, s32[]{:S(2)}) async-start(s8[13631488]{0:T(1024)(128)(4,1)} %bitcast.6), calls=%async_computation.12 | async-start | bytes 2097152
Sparse Core Ops, SparseCore 0:
  11.4 91.6 reduce-scatter.3
  106.6 88.8 reduce-scatter.5
  198.9 88.8 reduce-scatter.7
  321.2 72.7 all-gather.7
  396.3 70.8 all-gather.3
  469.5 70.8 all-gather.5
where the time goes:
time: 575 us
  waiting for transfers between devices  478 us (83%)
  other arithmetic  29.7 us (5%)
  local copies, waits for them, and re-layouts  27.3 us (5%)
  blocking collectives  22.2 us (4%)
  between operations  16.8 us (3%)
    reduce_scatter x3, waiting for transfers between devices, step(): lax.psum_scatter(t[0], 'dp', scatter_dimension=1, tiled=True)  271 us
    all_gather x3, waiting for transfers between devices, step(): whole = [lax.all_gather(one[0], 'dp', axis=1, tiled=True) for one in new]  205 us
    unnamed x17, local copies, waits for them, and re-layouts  27.3 us
    psum x1, blocking collectives, step(): squares = lax.psum(sum((jnp.sum(g * g) for g in gradients)), 'dp')  22.2 us
    convert_element_type x3, other arithmetic, adamw(): return ((w - 0.02 * step).astype(jnp.bfloat16), m, v)  20.9 us
  transfers between devices with their start and end apart: 6, of which 6 were waited for; matrix products, arithmetic and copies ran while one was open for 3% of the time, Pallas kernels for 0%

commit v1 on v0

v1 whole, which is shorter than its diff:
```python
import functools

import jax
import jax.numpy as jnp
from jax import lax
from jax.experimental import pallas as pl
from jax.experimental.pallas import tpu as pltpu
from jax.sharding import PartitionSpec as P

MESH = pl.DeviceIdType.MESH
DIAGONAL, FIRST, SECOND, OWN = range(4)
FLIPS = (((1, 1), (1, 0), (0, 1), (0, 0)), ((1, 1), (0, 1), (1, 0), (0, 0)))
LAYERS = 2
SPLIT = 2


def flipped(fx, fy, fc):
    me = lax.axis_index("dp")
    x, y, c = me // 4, (me // 2) % 2, me % 2
    return (1 - x if fx else x) * 4 + (1 - y if fy else y) * 2 + (1 - c if fc else c)


def scatter_kernel(count, *refs):
    g, out, factor_ref = refs[:3], refs[3:6], refs[6]
    own, par, r1, r2 = refs[7:10], refs[10:13], refs[13:16], refs[16:19]
    squares, own_sem, psend_sem, precv_sem, send_sem, r1_sem, r2_sem, out_sem, ssend_sem, srecv_sem = refs[19:]
    me = lax.axis_index("dp")
    pieces = [(w, s, layer) for w in range(3) for s in range(SPLIT) for layer in range(LAYERS)]

    def rows(w):
        return own[w].shape[2] // SPLIT

    def span(w, s):
        return pl.ds(s * rows(w), rows(w))

    def source(w, layer, s, device):
        return g[w].at[0, layer, pl.ds(pl.multiple_of(device * (rows(w) * SPLIT) + s * rows(w), 16), rows(w))]

    def load(w, layer, whose, s):
        return pltpu.make_async_copy(
            source(w, layer, s, flipped(*FLIPS[layer][whose], 0)), own[w].at[layer, whose, span(w, s)], own_sem.at[w, layer, whose, s]
        )

    def swap(w, layer, whose, s):
        return pltpu.make_async_remote_copy(
            source(w, layer, s, flipped(*FLIPS[layer][whose], 1)),
            par[w].at[layer, whose, span(w, s)],
            psend_sem.at[w, layer, whose, s],
            precv_sem.at[w, layer, whose, s],
            device_id={"dp": flipped(0, 0, 1)},
            device_id_type=MESH,
        )

    def send(w, layer, whose, s):
        src = own[w].at[layer, whose, span(w, s)]
        if whose == SECOND:
            dst, sem, link = r2[w].at[layer, span(w, s)], r2_sem.at[w, layer, s], SECOND
        else:
            slot = 0 if whose == DIAGONAL else 1
            dst, sem, link = r1[w].at[layer, slot, span(w, s)], r1_sem.at[w, layer, slot, s], FIRST
        return pltpu.make_async_remote_copy(
            src, dst, send_sem.at[w, layer, whose, s], sem, device_id={"dp": flipped(*FLIPS[layer][link], 0)}, device_id_type=MESH
        )

    def result(w, layer, s):
        return pltpu.make_async_copy(own[w].at[layer, OWN, span(w, s)], out[w].at[layer, span(w, s)], out_sem.at[w, layer, s])

    def add(w, layer, whose, s, squares_so_far=None):
        columns = own[w].shape[3]
        width = columns // 2
        others = [par[w].at[layer, whose]]
        if whose == SECOND:
            others.append(r1[w].at[layer, 0])
        if whose == OWN:
            others += [r1[w].at[layer, 1], r2[w].at[layer]]
        mine = own[w].at[layer, whose]

        def body(i, so_far):
            at = pl.ds(pl.multiple_of(s * rows(w) + i * 16, 16), 16)
            for half in range(2):
                cut = pl.ds(half * width, width)
                total = mine[at, cut].astype(jnp.float32)
                for other in others:
                    total += other[at, cut].astype(jnp.float32)
                rounded = total.astype(jnp.bfloat16)
                mine[at, cut] = rounded
                if so_far is not None:
                    wide = rounded.astype(jnp.float32)
                    wide = wide * wide
                    for k in range(width // 128):
                        so_far = so_far + wide[:, k * 128 : (k + 1) * 128]
            return so_far

        return lax.fori_loop(0, rows(w) // 16, body, squares_so_far)

    for w, s, layer in pieces:
        load(w, layer, DIAGONAL, s).start()
    barrier = pltpu.get_barrier_semaphore()
    for other in range(1, 8):
        pl.semaphore_signal(barrier, inc=1, device_id={"dp": flipped(other // 4, (other // 2) % 2, other % 2)}, device_id_type=MESH)
    pl.semaphore_wait(barrier, 7)
    for whose in range(4):
        for w, s, layer in pieces:
            if whose != DIAGONAL:
                load(w, layer, whose, s).start()
            swap(w, layer, whose, s).start()

    so_far = jnp.zeros((16, 128), jnp.float32)
    for whose in range(4):
        for w, s, layer in pieces:
            load(w, layer, whose, s).wait()
            swap(w, layer, whose, s).wait_recv()
            if whose == SECOND:
                send(w, layer, DIAGONAL, s).wait_recv()
            if whose == OWN:
                send(w, layer, FIRST, s).wait_recv()
                send(w, layer, SECOND, s).wait_recv()
                so_far = add(w, layer, whose, s, so_far)
                result(w, layer, s).start()
            else:
                add(w, layer, whose, s)
                send(w, layer, whose, s).start()

    squares[me] = so_far[:8] + so_far[8:]

    def tell(other):
        return pltpu.make_async_remote_copy(
            squares.at[me],
            squares.at[me],
            ssend_sem.at[other],
            srecv_sem.at[other],
            device_id={"dp": flipped(other // 4, (other // 2) % 2, other % 2)},
            device_id_type=MESH,
        )

    for other in range(1, 8):
        tell(other).start()
    for other in range(1, 8):
        tell(other).wait_recv()
    total = squares[0]
    for device in range(1, 8):
        total = total + squares[device]
    total = jnp.sum(jnp.sum(total, axis=1, keepdims=True), axis=0, keepdims=True)
    factor = jnp.minimum(1.0, 0.5 * lax.rsqrt(total / count + 1e-30))
    factor_ref[...] = jnp.broadcast_to(factor, factor_ref.shape)

    for other in range(1, 8):
        tell(other).wait_send()
    for w, s, layer in pieces:
        result(w, layer, s).wait()
        for whose in range(4):
            swap(w, layer, whose, s).wait_send()
            if whose != OWN:
                send(w, layer, whose, s).wait_send()


def scatter(terms, blocks, count):
    shapes = [b.shape[1:] for b in blocks]

    def buffers(*lead):
        return [pltpu.VMEM((LAYERS, *lead, *shape), jnp.bfloat16) for shape in shapes]

    dma = pltpu.SemaphoreType.DMA
    any_space = pl.BlockSpec(memory_space=pl.ANY)
    return pl.pallas_call(
        functools.partial(scatter_kernel, count),
        name="scatter",
        out_shape=[jax.ShapeDtypeStruct(b.shape, jnp.bfloat16) for b in blocks] + [jax.ShapeDtypeStruct((8, 128), jnp.float32)],
        in_specs=[any_space] * 3,
        out_specs=[any_space] * 3 + [pl.BlockSpec(memory_space=pltpu.VMEM)],
        scratch_shapes=[
            *buffers(4),
            *buffers(4),
            *buffers(2),
            *buffers(),
            pltpu.VMEM((8, 8, 128), jnp.float32),
            dma((3, LAYERS, 4, SPLIT)),
            dma((3, LAYERS, 4, SPLIT)),
            dma((3, LAYERS, 4, SPLIT)),
            dma((3, LAYERS, 3, SPLIT)),
            dma((3, LAYERS, 2, SPLIT)),
            dma((3, LAYERS, SPLIT)),
            dma((3, LAYERS, SPLIT)),
            dma((8,)),
            dma((8,)),
        ],
        compiler_params=pltpu.CompilerParams(collective_id=0, has_side_effects=True, vmem_limit_bytes=60 * 1024 * 1024),
    )(*terms)


def adamw_kernel(me_ref, factor_ref, g_ref, w_ref, m_ref, v_ref, first_ref, second_ref, new_m_ref, new_v_ref):
    factor = factor_ref[0:1, 0:1]
    for layer, new_w_ref in enumerate((first_ref, second_ref)):
        g = g_ref[layer].astype(jnp.float32) * factor
        m = 0.9 * m_ref[layer] + 0.1 * g
        v = 0.95 * v_ref[layer] + 0.05 * g * g
        w = w_ref[layer].astype(jnp.float32)
        step = m * lax.rsqrt(v + 1e-8) + 0.1 * w
        new_w_ref[...] = (w - 0.02 * step).astype(jnp.bfloat16)
        new_m_ref[layer] = m
        new_v_ref[layer] = v


def adamw(me, factor, g, w, m, v):
    _, rows, columns = m.shape
    steps = 4
    cut = rows // steps
    block = pl.BlockSpec((LAYERS, cut, columns), lambda i, me: (0, i, 0))
    flat = pl.BlockSpec((cut, columns), lambda i, me: (i, 0))
    return pl.pallas_call(
        adamw_kernel,
        name="adamw",
        out_shape=[jax.ShapeDtypeStruct((rows, columns), jnp.bfloat16)] * 2 + [jax.ShapeDtypeStruct(m.shape, jnp.float32)] * 2,
        grid_spec=pltpu.PrefetchScalarGridSpec(
            num_scalar_prefetch=1,
            grid=(steps,),
            in_specs=[
                pl.BlockSpec((8, 128), lambda i, me: (0, 0)),
                block,
                pl.BlockSpec((LAYERS, cut, columns), lambda i, me: (0, me[0] * steps + i, 0)),
                block,
                block,
            ],
            out_specs=[flat, flat, block, block],
        ),
        compiler_params=pltpu.CompilerParams(vmem_limit_bytes=40 * 2**20),
        cost_estimate=pl.CostEstimate(flops=20 * m.size * 100, bytes_accessed=22 * m.size, transcendentals=m.size),
    )(me, factor, g, w, m, v)


def join(where, layer, pieces, shape, so_far):
    rows, columns = pieces[0].shape
    n = len(pieces)
    extra = [] if so_far is None else [so_far]

    def kernel(where_ref, *refs):
        parts = refs[:n]
        out, held, in_sem, out_sem = refs[-4:]

        def take(k):
            return pltpu.make_async_copy(parts[k], held.at[k], in_sem.at[k])

        def put(k):
            at = pl.ds(pl.multiple_of(where_ref[k] * rows, 16), rows)
            return pltpu.make_async_copy(held.at[k], out.at[layer, at], out_sem.at[k])

        for k in range(n):
            take(k).start()
        for k in range(n):
            take(k).wait()
            put(k).start()
        for k in range(n):
            put(k).wait()

    any_space = pl.BlockSpec(memory_space=pl.ANY)
    return pl.pallas_call(
        kernel,
        name="join",
        out_shape=jax.ShapeDtypeStruct(shape, jnp.bfloat16),
        in_specs=[pl.BlockSpec(memory_space=pltpu.SMEM)] + [any_space] * (n + len(extra)),
        out_specs=any_space,
        scratch_shapes=[pltpu.VMEM((n, rows, columns), jnp.bfloat16), pltpu.SemaphoreType.DMA((n,)), pltpu.SemaphoreType.DMA((n,))],
        input_output_aliases={n + 1: 0} if extra else {},
        compiler_params=pltpu.CompilerParams(vmem_limit_bytes=20 * 2**20),
        cost_estimate=pl.CostEstimate(flops=100 * n * rows * columns, bytes_accessed=4 * n * rows * columns, transcendentals=0),
    )(where, *pieces, *extra)


def solution(mesh):
    def step(*arrays):
        terms, weights, m, v = (arrays[i : i + 3] for i in (0, 3, 6, 9))
        count = float(sum(w.size for w in weights))
        *gradients, factor = scatter(terms, m, count)
        me = lax.axis_index("dp")
        me_array = jnp.full((1,), me, jnp.int32)

        def hop(array, fx, fy, fc):
            return lax.ppermute(array, "dp", [(d, d ^ (4 * fx + 2 * fy + fc)) for d in range(8)])

        new = [adamw(me_array, factor, *one) for one in zip(gradients, weights, m, v, strict=True)]
        whole = []
        for i, (first, second, *_) in enumerate(new):
            result = None
            for layer, mine in enumerate((first, second)):
                near = FLIPS[layer][FIRST], FLIPS[layer][SECOND]
                one = hop(mine, *near[0], 0)
                two = hop(mine, *near[1], 0)
                both = hop(one, *near[1], 0)
                here = [mine, one, two, both]
                there = [hop(a, 0, 0, 1) for a in here]
                flips = [(0, 0), near[0], near[1], (1, 1)]
                where = jnp.stack([flipped(*f, fc) for fc in (0, 1) for f in flips]).astype(jnp.int32)
                result = join(where, layer, here + there, weights[i].shape, result)
            whole.append(result)
        return (*whole, *(one[2] for one in new), *(one[3] for one in new))

    all_of, cut = P(None, None, None), P(None, "dp", None)
    return jax.shard_map(
        step,
        mesh=mesh,
        in_specs=(P(("rep", "dp"), None, None, None),) * 3 + (all_of,) * 3 + (cut,) * 6,
        out_specs=(P("rep", None, None),) * 3 + (P("rep", "dp", None),) * 6,
        check_vma=False,
    )
```

time: 575 us -> 420 us (0.73)
  waiting for transfers between devices: 478 us -> 131 us
  Pallas kernels: 0 us -> 233 us
  other arithmetic: 29.7 us -> 0 us
  blocking collectives: 22.2 us -> 0 us
  starting transfers between devices: 0.24 us -> 16.2 us
  between operations: 16.8 us -> 1.26 us
  local copies, waits for them, and re-layouts: 27.3 us -> 37.4 us
    reduce_scatter x3 -> x0, waiting for transfers between devices: 271 us -> none  [step(): lax.psum_scatter(t[0], 'dp', scatter_dimension=1, tiled=True)]
    pallas_call x0 -> x10, Pallas kernels: none -> 233 us  [the longest x1 180 us: scatter(): pl.pallas_call(functools.partial(scatter_kernel, count), name='scatter',...]
    all_gather x3 -> x0, waiting for transfers between devices: 205 us -> none  [step(): whole = [lax.all_gather(one[0], 'dp', axis=1, tiled=True) for one in new]]
    ppermute x0 -> x42, waiting for transfers between devices: none -> 131 us  [hop(): lax.ppermute(array, 'dp', [(d, d ^ 4 * fx + 2 * fy + fc) for d in range(8)])]
    psum x1 -> x0, blocking collectives: 22.2 us -> none  [step(): squares = lax.psum(sum((jnp.sum(g * g) for g in gradients)), 'dp')]
    convert_element_type x3 -> x0, other arithmetic: 20.9 us -> none  [adamw(): return ((w - 0.02 * step).astype(jnp.bfloat16), m, v)]
    ppermute x0 -> x42, starting transfers between devices: none -> 16.2 us  [hop(): lax.ppermute(array, 'dp', [(d, d ^ 4 * fx + 2 * fy + fc) for d in range(8)])]
    unnamed x17 -> x144, local copies, waits for them, and re-layouts: 27.3 us -> 37.2 us
  transfers between devices with their start and end apart: 6 -> 42, of which waited for: 6 -> 11; matrix products, arithmetic and copies ran while one was open for 3% -> 0% of each run, Pallas kernels for 0% -> 9%
where the time goes in v1:
time: 420 us
  Pallas kernels  233 us (55%)
  waiting for transfers between devices  131 us (31%)
  local copies, waits for them, and re-layouts  37.4 us (9%)
  starting transfers between devices  16.2 us (4%)
    pallas_call x1, Pallas kernels, scatter(): pl.pallas_call(functools.partial(scatter_kernel, count), name='scatter',...  180 us
    ppermute x42, waiting for transfers between devices, hop(): lax.ppermute(array, 'dp', [(d, d ^ 4 * fx + 2 * fy + fc) for d in range(8)])  131 us
    unnamed x144, local copies, waits for them, and re-layouts  37.2 us
    pallas_call x6, Pallas kernels, join(): pl.pallas_call(kernel, name='join', out_shape=jax.ShapeDtypeStruct(shape,...  30.1 us
    pallas_call x3, Pallas kernels, adamw(): pl.pallas_call(adamw_kernel, name='adamw', out_shape=[jax.ShapeDtypeStruc...  23.6 us
    ppermute x42, starting transfers between devices, hop(): lax.ppermute(array, 'dp', [(d, d ^ 4 * fx + 2 * fy + fc) for d in range(8)])  16.2 us
  transfers between devices with their start and end apart: 42, of which 11 were waited for; matrix products, arithmetic and copies ran while one was open for 0% of the time, Pallas kernels for 9%

profile of v1, /device:TPU:0, one launch (start us, length us, event | category | flops | bytes accessed | tf_op | source)
XLA Modules:
  0.0 419.7 jit_solution(8761953021291903080)
XLA Ops:
  0.7 179.8 %scatter.1 = (bf16[2,128,3328]{2,1,0:T(8,128)(2,1)}, bf16[2,128,3328]{2,1,0:T(8,128)(2,1)}, bf16[2,416,1024]{2,1,0:T(8,128)(2,1)}, f32[8,128]{1,0:T(8,128)}) custom-call(bf16[1,2,1024,3328]{3,2,1,0:T(8,128)(2,1)} %refs_0_.1, bf16[1,2,1024,3328]{3,2,1,0:T(8,128)(2,1)} %refs_1_.1, bf16[1,2,3328,1024]{3,2,1,0:T(8,128)(2,1)} %refs_2_.1), custom_call_target="tpu_custom_call" | custom-call | tf_op jit(solution)/shard_map/scatter/pallas_call | solution.py:165
  180.5 2.0 copy-done.1
  182.4 1.5 copy-done.8
  184.6 8.4 %adamw.5 = (bf16[416,1024]{1,0:T(8,128)(2,1)}, bf16[416,1024]{1,0:T(8,128)(2,1)}, f32[2,416,1024]{2,1,0:T(8,128)}, f32[2,416,1024]{2,1,0:T(8,128)}) custom-call(s32[1]{0:T(128)} %bitcast.8.me_ref, f32[8,128]{1,0:T(8,128)S(1)} %copy-done.71, bf16[2,416,1024]{2,1,0:T(8,128)(2,1)S(1)} %copy-done.8, bf16[2,3328,1024]{2,1,0:T(8,128)(2,1)} %w_ref.5, ...), custom_call_target="tpu_custom_call" | custom-call | flops 1703936000 | bytes 18743296 | tf_op jit(solution)/shard_map/adamw/pallas_call | solution.py:210
  193.0 1.5 collective-permute-start.35
  195.0 1.5 collective-permute-start.28
  197.1 8.2 %adamw.4 = (bf16[128,3328]{1,0:T(8,128)(2,1)}, bf16[128,3328]{1,0:T(8,128)(2,1)S(1)}, f32[2,128,3328]{2,1,0:T(8,128)}, f32[2,128,3328]{2,1,0:T(8,128)}) custom-call(s32[1]{0:T(128)} %bitcast.8.me_ref, f32[8,128]{1,0:T(8,128)S(1)} %copy-done.71, bf16[2,128,3328]{2,1,0:T(8,128)(2,1)S(1)} %copy-done.7, bf16[2,1024,3328]{2,1,0:T(8,128)(2,1)} %w_ref.4, ...), custom_call_target="tpu_custom_call" | custom-call | flops 1703936000 | bytes 18743296 | tf_op jit(solution)/shard_map/adamw/pallas_call | solution.py:210
  205.2 9.8 %collective-permute-done.35.refs_1_ = bf16[416,1024]{1,0:T(8,128)(2,1)S(1)} collective-permute-done((bf16[416,1024]{1,0:T(8,128)(2,1)}, bf16[416,1024]{1,0:T(8,128)(2,1)S(1)}, u32[]{:S(2)}, u32[]{:S(2)}) %collective-permute-start.35) | collective-permute-done | bytes 852000 | tf_op jit(solution)/shard_map/ppermute | solution.py:278
  215.0 1.5 collective-permute-done.36.refs_2_
  217.6 17.2 %collective-permute-done.28.refs_1_ = bf16[416,1024]{1,0:T(8,128)(2,1)S(1)} collective-permute-done((bf16[416,1024]{1,0:T(8,128)(2,1)}, bf16[416,1024]{1,0:T(8,128)(2,1)S(1)}, u32[]{:S(2)}, u32[]{:S(2)}) %collective-permute-start.28) | collective-permute-done | bytes 852000 | tf_op jit(solution)/shard_map/ppermute | solution.py:278
  235.8 15.7 %collective-permute-done.21.refs_1_ = bf16[128,3328]{1,0:T(8,128)(2,1)S(1)} collective-permute-done((bf16[128,3328]{1,0:T(8,128)(2,1)}, bf16[128,3328]{1,0:T(8,128)(2,1)S(1)}, u32[]{:S(2)}, u32[]{:S(2)}) %collective-permute-start.21) | collective-permute-done | bytes 852000 | tf_op jit(solution)/shard_map/ppermute | solution.py:278
  251.5 7.0 %adamw.3 = (bf16[128,3328]{1,0:T(8,128)(2,1)S(1)}, bf16[128,3328]{1,0:T(8,128)(2,1)}, f32[2,128,3328]{2,1,0:T(8,128)}, f32[2,128,3328]{2,1,0:T(8,128)}) custom-call(s32[1]{0:T(128)} %bitcast.8.me_ref, f32[8,128]{1,0:T(8,128)S(1)} %copy-done.71, bf16[2,128,3328]{2,1,0:T(8,128)(2,1)S(1)} %copy-done.6, bf16[2,1024,3328]{2,1,0:T(8,128)(2,1)} %w_ref.3, ...), custom_call_target="tpu_custom_call" | custom-call | flops 1703936000 | bytes 18743296 | tf_op jit(solution)/shard_map/adamw/pallas_call | solution.py:210
  258.5 1.5 collective-permute-start.7
  260.0 0.9 copy-done.25
  261.5 9.7 %collective-permute-done.14.refs_1_ = bf16[128,3328]{1,0:T(8,128)(2,1)S(1)} collective-permute-done((bf16[128,3328]{1,0:T(8,128)(2,1)S(1)}, bf16[128,3328]{1,0:T(8,128)(2,1)S(1)}, u32[]{:S(2)}, u32[]{:S(2)}) %collective-permute-start.14) | collective-permute-done | bytes 852000 | tf_op jit(solution)/shard_map/ppermute | solution.py:278
  272.7 0.9 copy-done.21
  274.2 13.9 %collective-permute-done.7.refs_1_ = bf16[128,3328]{1,0:T(8,128)(2,1)S(1)} collective-permute-done((bf16[128,3328]{1,0:T(8,128)(2,1)S(1)}, bf16[128,3328]{1,0:T(8,128)(2,1)S(1)}, u32[]{:S(2)}, u32[]{:S(2)}) %collective-permute-start.7) | collective-permute-done | bytes 852000 | tf_op jit(solution)/shard_map/ppermute | solution.py:278
  288.6 0.9 collective-permute-done.8.refs_2_
  289.5 1.0 copy-done.33
  291.0 16.9 %collective-permute-done.refs_1_ = bf16[128,3328]{1,0:T(8,128)(2,1)} collective-permute-done((bf16[128,3328]{1,0:T(8,128)(2,1)}, bf16[128,3328]{1,0:T(8,128)(2,1)}, u32[]{:S(2)}, u32[]{:S(2)}) %collective-permute-start) | collective-permute-done | bytes 852000 | tf_op jit(solution)/shard_map/ppermute | solution.py:278
  308.4 16.5 %collective-permute-done.37.refs_3_ = bf16[416,1024]{1,0:T(8,128)(2,1)S(1)} collective-permute-done((bf16[416,1024]{1,0:T(8,128)(2,1)S(1)}, bf16[416,1024]{1,0:T(8,128)(2,1)S(1)}, u32[]{:S(2)}, u32[]{:S(2)}) %collective-permute-start.37) | collective-permute-done | bytes 852000 | tf_op jit(solution)/shard_map/ppermute | solution.py:278
  324.9 1.0 copy-done.43
  330.2 0.9 copy-done.41
  331.1 1.0 copy-done.15
  332.1 15.1 %collective-permute-done.23.refs_3_ = bf16[128,3328]{1,0:T(8,128)(2,1)S(1)} collective-permute-done((bf16[128,3328]{1,0:T(8,128)(2,1)S(1)}, bf16[128,3328]{1,0:T(8,128)(2,1)S(1)}, u32[]{:S(2)}, u32[]{:S(2)}) %collective-permute-start.23) | collective-permute-done | bytes 852000 | tf_op jit(solution)/shard_map/ppermute | solution.py:278
  351.9 1.0 copy-done.31
  354.3 0.9 copy-done.51
  355.2 0.9 copy-done.39
  356.2 14.2 %collective-permute-done.9.refs_3_ = bf16[128,3328]{1,0:T(8,128)(2,1)S(1)} collective-permute-done((bf16[128,3328]{1,0:T(8,128)(2,1)S(1)}, bf16[128,3328]{1,0:T(8,128)(2,1)S(1)}, u32[]{:S(2)}, u32[]{:S(2)}) %collective-permute-start.9) | collective-permute-done | bytes 852000 | tf_op jit(solution)/shard_map/ppermute | solution.py:278
  370.4 0.9 copy-done.35
  371.3 0.9 copy-done.59
  372.8 0.9 copy-done.49
  373.7 0.9 copy-done.61
  374.6 0.9 copy-done.57
  379.3 0.9 copy-done.67
  380.9 1.2 copy-done.10
  382.1 1.2 copy-done.12
  383.2 1.2 copy-done.14
  384.4 1.2 copy-done.40
  385.5 1.2 copy-done.44
  386.7 1.2 copy-done.46
  387.9 1.2 copy-done.66
  389.1 4.9 %join.10.refs_8_ = bf16[2,3328,1024]{2,1,0:T(8,128)(2,1)} custom-call(s32[8]{0:T(128)S(1)} %stack.29.where_ref, bf16[416,1024]{1,0:T(8,128)(2,1)} %get-tuple-element.34.refs_0_, bf16[416,1024]{1,0:T(8,128)(2,1)S(1)} %copy-done.10, bf16[416,1024]{1,0:T(8,128)(2,1)S(1)} %copy-done.12, bf16[416,1024]{1,0:T(8,128)(2,1)S(1)} %copy-done.40, ...), custom_call_target="tpu_custom_call" | custom-call | flops 340787200 | bytes 13631488 | tf_op jit(solution)/shard_map/join/pallas_call | solution.py:256
  394.1 5.0 %join.8.refs_8_ = bf16[2,1024,3328]{2,1,0:T(8,128)(2,1)} custom-call(s32[8]{0:T(128)S(1)} %stack.29.where_ref, bf16[128,3328]{1,0:T(8,128)(2,1)} %get-tuple-element.31.refs_0_, bf16[128,3328]{1,0:T(8,128)(2,1)S(1)} %copy-done.20, bf16[128,3328]{1,0:T(8,128)(2,1)S(1)} %copy-done.24, bf16[128,3328]{1,0:T(8,128)(2,1)S(1)} %copy-done.50, ...), custom_call_target="tpu_custom_call" | custom-call | flops 340787200 | bytes 13631488 | tf_op jit(solution)/shard_map/join/pallas_call | solution.py:256
  399.2 4.6 %join.6.refs_8_ = bf16[2,1024,3328]{2,1,0:T(8,128)(2,1)} custom-call(s32[8]{0:T(128)S(1)} %stack.29.where_ref, bf16[128,3328]{1,0:T(8,128)(2,1)S(1)} %copy-done.28, bf16[128,3328]{1,0:T(8,128)(2,1)S(1)} %copy-done.30, bf16[128,3328]{1,0:T(8,128)(2,1)S(1)} %copy-done.32, bf16[128,3328]{1,0:T(8,128)(2,1)S(1)} %copy-done.58, bf16[128,3328]{1,0:T(8,128)(2,1)S(1)} %copy-done.34, ...), custom_call_target="tpu_custom_call" | custom-call | flops 340787200 | bytes 13631488 | tf_op jit(solution)/shard_map/join/pallas_call | solution.py:256
  403.9 4.9 %join.11 = bf16[2,3328,1024]{2,1,0:T(8,128)(2,1)} custom-call(s32[8]{0:T(128)S(1)} %stack.28.where_ref, bf16[416,1024]{1,0:T(8,128)(2,1)} %get-tuple-element.33.refs_0_, bf16[416,1024]{1,0:T(8,128)(2,1)S(1)} %collective-permute-done.28.refs_1_, bf16[416,1024]{1,0:T(8,128)(2,1)S(1)} %collective-permute-done.29.refs_2_, ...), custom_call_target="tpu_custom_call", output_to_operand_aliasing={{}: (9, {})} | custom-call | flops 340787200 | bytes 13631488 | tf_op jit(solution)/shard_map/join/pallas_call | solution.py:256
  408.9 4.3 %join.9 = bf16[2,1024,3328]{2,1,0:T(8,128)(2,1)} custom-call(s32[8]{0:T(128)S(1)} %stack.28.where_ref, bf16[128,3328]{1,0:T(8,128)(2,1)S(1)} %get-tuple-element.30.refs_0_, bf16[128,3328]{1,0:T(8,128)(2,1)S(1)} %copy-done.16, bf16[128,3328]{1,0:T(8,128)(2,1)S(1)} %copy-done.18, ...), custom_call_target="tpu_custom_call", output_to_operand_aliasing={{}: (9, {})} | custom-call | flops 340787200 | bytes 13631488 | tf_op jit(solution)/shard_map/join/pallas_call | solution.py:256
  413.3 6.3 %join.7 = bf16[2,1024,3328]{2,1,0:T(8,128)(2,1)} custom-call(s32[8]{0:T(128)S(1)} %stack.28.where_ref, bf16[128,3328]{1,0:T(8,128)(2,1)} %get-tuple-element.27.refs_0_, bf16[128,3328]{1,0:T(8,128)(2,1)} %collective-permute-done.refs_1_, bf16[128,3328]{1,0:T(8,128)(2,1)} %collective-permute-done.1.refs_2_, ...), custom_call_target="tpu_custom_call", output_to_operand_aliasing={{}: (9, {})} | custom-call | flops 340787200 | bytes 13631488 | tf_op jit(solution)/shard_map/join/pallas_call | solution.py:256
  (192 shorter events, 23.7 us)
Async XLA Ops:
  0.6 179.8 %copy-start = (f32[2,416,1024]{2,1,0:T(8,128)S(1)}, f32[2,416,1024]{2,1,0:T(8,128)}, u32[]{:S(2)}) copy-start(f32[2,416,1024]{2,1,0:T(8,128)} %m_ref.5) | copy-start | bytes 10223620
  193.0 22.0 %collective-permute-start.35 = (bf16[416,1024]{1,0:T(8,128)(2,1)}, bf16[416,1024]{1,0:T(8,128)(2,1)S(1)}, u32[]{:S(2)}, u32[]{:S(2)}) collective-permute-start(bf16[416,1024]{1,0:T(8,128)(2,1)} %get-tuple-element.34.refs_0_), channel_id=1, source_target_pairs={{0,4},{1,5},{2,6},{3,7},{4,0},{5,1},{6,2},{7,3}} | collective-permute-start | bytes 2555912 | tf_op jit(solution)/shard_map/ppermute | solution.py:278
  194.4 22.0 %collective-permute-start.36 = (bf16[416,1024]{1,0:T(8,128)(2,1)}, bf16[416,1024]{1,0:T(8,128)(2,1)S(1)}, u32[]{:S(2)}, u32[]{:S(2)}) collective-permute-start(bf16[416,1024]{1,0:T(8,128)(2,1)} %get-tuple-element.34.refs_0_), channel_id=1, source_target_pairs={{0,2},{1,3},{2,0},{3,1},{4,6},{5,7},{6,4},{7,5}} | collective-permute-start | bytes 2555912 | tf_op jit(solution)/shard_map/ppermute | solution.py:278
  195.0 22.0 %collective-permute-start.38 = (bf16[416,1024]{1,0:T(8,128)(2,1)}, bf16[416,1024]{1,0:T(8,128)(2,1)S(1)}, u32[]{:S(2)}, u32[]{:S(2)}) collective-permute-start(bf16[416,1024]{1,0:T(8,128)(2,1)} %get-tuple-element.34.refs_0_), channel_id=1, source_target_pairs={{0,1},{1,0},{2,3},{3,2},{4,5},{5,4},{6,7},{7,6}} | collective-permute-start | bytes 2555912 | tf_op jit(solution)/shard_map/ppermute | solution.py:278
  195.0 39.7 %collective-permute-start.28 = (bf16[416,1024]{1,0:T(8,128)(2,1)}, bf16[416,1024]{1,0:T(8,128)(2,1)S(1)}, u32[]{:S(2)}, u32[]{:S(2)}) collective-permute-start(bf16[416,1024]{1,0:T(8,128)(2,1)} %get-tuple-element.33.refs_0_), channel_id=1, source_target_pairs={{0,2},{1,3},{2,0},{3,1},{4,6},{5,7},{6,4},{7,5}} | collective-permute-start | bytes 2555912 | tf_op jit(solution)/shard_map/ppermute | solution.py:278
  196.5 38.3 %collective-permute-start.29 = (bf16[416,1024]{1,0:T(8,128)(2,1)}, bf16[416,1024]{1,0:T(8,128)(2,1)S(1)}, u32[]{:S(2)}, u32[]{:S(2)}) collective-permute-start(bf16[416,1024]{1,0:T(8,128)(2,1)} %get-tuple-element.33.refs_0_), channel_id=1, source_target_pairs={{0,4},{1,5},{2,6},{3,7},{4,0},{5,1},{6,2},{7,3}} | collective-permute-start | bytes 2555912 | tf_op jit(solution)/shard_map/ppermute | solution.py:278
  197.0 54.5 %copy-start.4 = (f32[2,128,3328]{2,1,0:T(8,128)S(1)}, f32[2,128,3328]{2,1,0:T(8,128)}, u32[]{:S(2)}) copy-start(f32[2,128,3328]{2,1,0:T(8,128)} %m_ref.3) | copy-start | bytes 10223620
  197.0 54.5 %copy-start.5 = (f32[2,128,3328]{2,1,0:T(8,128)S(1)}, f32[2,128,3328]{2,1,0:T(8,128)}, u32[]{:S(2)}) copy-start(f32[2,128,3328]{2,1,0:T(8,128)} %v_ref.3) | copy-start | bytes 10223620
  215.0 74.5 %copy-start.9 = (bf16[416,1024]{1,0:T(8,128)(2,1)}, bf16[416,1024]{1,0:T(8,128)(2,1)S(1)}, u32[]{:S(2)}) copy-start(bf16[416,1024]{1,0:T(8,128)(2,1)S(1)} %collective-permute-done.35.refs_1_) | copy-start | bytes 2555908
  215.0 20.3 %collective-permute-start.31 = (bf16[416,1024]{1,0:T(8,128)(2,1)}, bf16[416,1024]{1,0:T(8,128)(2,1)S(1)}, u32[]{:S(2)}, u32[]{:S(2)}) collective-permute-start(bf16[416,1024]{1,0:T(8,128)(2,1)} %get-tuple-element.33.refs_0_), channel_id=1, source_target_pairs={{0,1},{1,0},{2,3},{3,2},{4,5},{5,4},{6,7},{7,6}} | collective-permute-start | bytes 2555912 | tf_op jit(solution)/shard_map/ppermute | solution.py:278
  216.5 73.0 %copy-start.11 = (bf16[416,1024]{1,0:T(8,128)(2,1)}, bf16[416,1024]{1,0:T(8,128)(2,1)S(1)}, u32[]{:S(2)}) copy-start(bf16[416,1024]{1,0:T(8,128)(2,1)S(1)} %collective-permute-done.36.refs_2_) | copy-start | bytes 2555908
  216.5 35.0 %collective-permute-start.21 = (bf16[128,3328]{1,0:T(8,128)(2,1)}, bf16[128,3328]{1,0:T(8,128)(2,1)S(1)}, u32[]{:S(2)}, u32[]{:S(2)}) collective-permute-start(bf16[128,3328]{1,0:T(8,128)(2,1)} %get-tuple-element.31.refs_0_), channel_id=1, source_target_pairs={{0,4},{1,5},{2,6},{3,7},{4,0},{5,1},{6,2},{7,3}} | collective-permute-start | bytes 2555912 | tf_op jit(solution)/shard_map/ppermute | solution.py:278
  217.0 41.5 %collective-permute-start.22 = (bf16[128,3328]{1,0:T(8,128)(2,1)}, bf16[128,3328]{1,0:T(8,128)(2,1)S(1)}, u32[]{:S(2)}, u32[]{:S(2)}) collective-permute-start(bf16[128,3328]{1,0:T(8,128)(2,1)} %get-tuple-element.31.refs_0_), channel_id=1, source_target_pairs={{0,2},{1,3},{2,0},{3,1},{4,6},{5,7},{6,4},{7,5}} | collective-permute-start | bytes 2555912 | tf_op jit(solution)/shard_map/ppermute | solution.py:278
  234.7 25.3 %collective-permute-start.24 = (bf16[128,3328]{1,0:T(8,128)(2,1)}, bf16[128,3328]{1,0:T(8,128)(2,1)S(1)}, u32[]{:S(2)}, u32[]{:S(2)}) collective-permute-start(bf16[128,3328]{1,0:T(8,128)(2,1)} %get-tuple-element.31.refs_0_), channel_id=1, source_target_pairs={{0,1},{1,0},{2,3},{3,2},{4,5},{5,4},{6,7},{7,6}} | collective-permute-start | bytes 2555912 | tf_op jit(solution)/shard_map/ppermute | solution.py:278
  234.7 36.5 %collective-permute-start.14 = (bf16[128,3328]{1,0:T(8,128)(2,1)S(1)}, bf16[128,3328]{1,0:T(8,128)(2,1)S(1)}, u32[]{:S(2)}, u32[]{:S(2)}) collective-permute-start(bf16[128,3328]{1,0:T(8,128)(2,1)S(1)} %get-tuple-element.30.refs_0_), channel_id=1, source_target_pairs={{0,2},{1,3},{2,0},{3,1},{4,6},{5,7},{6,4},{7,5}} | collective-permute-start | bytes 2555912 | tf_op jit(solution)/shard_map/ppermute | solution.py:278
  235.3 36.9 %collective-permute-start.15 = (bf16[128,3328]{1,0:T(8,128)(2,1)S(1)}, bf16[128,3328]{1,0:T(8,128)(2,1)S(1)}, u32[]{:S(2)}, u32[]{:S(2)}) collective-permute-start(bf16[128,3328]{1,0:T(8,128)(2,1)S(1)} %get-tuple-element.30.refs_0_), channel_id=1, source_target_pairs={{0,4},{1,5},{2,6},{3,7},{4,0},{5,1},{6,2},{7,3}} | collective-permute-start | bytes 2555912 | tf_op jit(solution)/shard_map/ppermute | solution.py:278
  251.5 74.9 %copy-start.19 = (bf16[128,3328]{1,0:T(8,128)(2,1)}, bf16[128,3328]{1,0:T(8,128)(2,1)S(1)}, u32[]{:S(2)}) copy-start(bf16[128,3328]{1,0:T(8,128)(2,1)S(1)} %collective-permute-done.21.refs_1_) | copy-start | bytes 2555908
  251.5 21.2 %collective-permute-start.17 = (bf16[128,3328]{1,0:T(8,128)(2,1)S(1)}, bf16[128,3328]{1,0:T(8,128)(2,1)S(1)}, u32[]{:S(2)}, u32[]{:S(2)}) collective-permute-start(bf16[128,3328]{1,0:T(8,128)(2,1)S(1)} %get-tuple-element.30.refs_0_), channel_id=1, source_target_pairs={{0,1},{1,0},{2,3},{3,2},{4,5},{5,4},{6,7},{7,6}} | collective-permute-start | bytes 2555912 | tf_op jit(solution)/shard_map/ppermute | solution.py:278
  258.5 29.5 %collective-permute-start.7 = (bf16[128,3328]{1,0:T(8,128)(2,1)S(1)}, bf16[128,3328]{1,0:T(8,128)(2,1)S(1)}, u32[]{:S(2)}, u32[]{:S(2)}) collective-permute-start(bf16[128,3328]{1,0:T(8,128)(2,1)S(1)} %get-tuple-element.28.refs_0_), channel_id=1, source_target_pairs={{0,4},{1,5},{2,6},{3,7},{4,0},{5,1},{6,2},{7,3}} | collective-permute-start | bytes 2555912 | tf_op jit(solution)/shard_map/ppermute | solution.py:278
  261.0 28.5 %collective-permute-start.8 = (bf16[128,3328]{1,0:T(8,128)(2,1)S(1)}, bf16[128,3328]{1,0:T(8,128)(2,1)S(1)}, u32[]{:S(2)}, u32[]{:S(2)}) collective-permute-start(bf16[128,3328]{1,0:T(8,128)(2,1)S(1)} %get-tuple-element.28.refs_0_), channel_id=1, source_target_pairs={{0,2},{1,3},{2,0},{3,1},{4,6},{5,7},{6,4},{7,5}} | collective-permute-start | bytes 2555912 | tf_op jit(solution)/shard_map/ppermute | solution.py:278
  271.2 18.3 %collective-permute-start.10 = (bf16[128,3328]{1,0:T(8,128)(2,1)S(1)}, bf16[128,3328]{1,0:T(8,128)(2,1)S(1)}, u32[]{:S(2)}, u32[]{:S(2)}) collective-permute-start(bf16[128,3328]{1,0:T(8,128)(2,1)S(1)} %get-tuple-element.28.refs_0_), channel_id=1, source_target_pairs={{0,1},{1,0},{2,3},{3,2},{4,5},{5,4},{6,7},{7,6}} | collective-permute-start | bytes 2555912 | tf_op jit(solution)/shard_map/ppermute | solution.py:278
  272.2 35.7 %collective-permute-start = (bf16[128,3328]{1,0:T(8,128)(2,1)}, bf16[128,3328]{1,0:T(8,128)(2,1)}, u32[]{:S(2)}, u32[]{:S(2)}) collective-permute-start(bf16[128,3328]{1,0:T(8,128)(2,1)} %get-tuple-element.27.refs_0_), channel_id=1, source_target_pairs={{0,2},{1,3},{2,0},{3,1},{4,6},{5,7},{6,4},{7,5}} | collective-permute-start | bytes 2555912 | tf_op jit(solution)/shard_map/ppermute | solution.py:278
  273.6 34.8 %collective-permute-start.1 = (bf16[128,3328]{1,0:T(8,128)(2,1)}, bf16[128,3328]{1,0:T(8,128)(2,1)}, u32[]{:S(2)}, u32[]{:S(2)}) collective-permute-start(bf16[128,3328]{1,0:T(8,128)(2,1)} %get-tuple-element.27.refs_0_), channel_id=1, source_target_pairs={{0,4},{1,5},{2,6},{3,7},{4,0},{5,1},{6,2},{7,3}} | collective-permute-start | bytes 2555912 | tf_op jit(solution)/shard_map/ppermute | solution.py:278
  288.0 36.9 %collective-permute-start.37 = (bf16[416,1024]{1,0:T(8,128)(2,1)S(1)}, bf16[416,1024]{1,0:T(8,128)(2,1)S(1)}, u32[]{:S(2)}, u32[]{:S(2)}) collective-permute-start(bf16[416,1024]{1,0:T(8,128)(2,1)S(1)} %collective-permute-done.35.refs_1_), channel_id=1, source_target_pairs={{0,2},{1,3},{2,0},{3,1},{4,6},{5,7},{6,4},{7,5}} | collective-permute-start | bytes 2555912 | tf_op jit(solution)/shard_map/ppermute | solution.py:278
  289.5 35.4 %collective-permute-start.39 = (bf16[416,1024]{1,0:T(8,128)(2,1)S(1)}, bf16[416,1024]{1,0:T(8,128)(2,1)S(1)}, u32[]{:S(2)}, u32[]{:S(2)}) collective-permute-start(bf16[416,1024]{1,0:T(8,128)(2,1)S(1)} %collective-permute-done.35.refs_1_), channel_id=1, source_target_pairs={{0,1},{1,0},{2,3},{3,2},{4,5},{5,4},{6,7},{7,6}} | collective-permute-start | bytes 2555912 | tf_op jit(solution)/shard_map/ppermute | solution.py:278
  290.5 35.9 %collective-permute-start.40 = (bf16[416,1024]{1,0:T(8,128)(2,1)S(1)}, bf16[416,1024]{1,0:T(8,128)(2,1)S(1)}, u32[]{:S(2)}, u32[]{:S(2)}) collective-permute-start(bf16[416,1024]{1,0:T(8,128)(2,1)S(1)} %collective-permute-done.36.refs_2_), channel_id=1, source_target_pairs={{0,1},{1,0},{2,3},{3,2},{4,5},{5,4},{6,7},{7,6}} | collective-permute-start | bytes 2555912 | tf_op jit(solution)/shard_map/ppermute | solution.py:278
  307.9 19.7 %collective-permute-start.30 = (bf16[416,1024]{1,0:T(8,128)(2,1)S(1)}, bf16[416,1024]{1,0:T(8,128)(2,1)S(1)}, u32[]{:S(2)}, u32[]{:S(2)}) collective-permute-start(bf16[416,1024]{1,0:T(8,128)(2,1)S(1)} %collective-permute-done.28.refs_1_), channel_id=1, source_target_pairs={{0,4},{1,5},{2,6},{3,7},{4,0},{5,1},{6,2},{7,3}} | collective-permute-start | bytes 2555912 | tf_op jit(solution)/shard_map/ppermute | solution.py:278
  308.4 20.3 %collective-permute-start.32 = (bf16[416,1024]{1,0:T(8,128)(2,1)S(1)}, bf16[416,1024]{1,0:T(8,128)(2,1)S(1)}, u32[]{:S(2)}, u32[]{:S(2)}) collective-permute-start(bf16[416,1024]{1,0:T(8,128)(2,1)S(1)} %collective-permute-done.28.refs_1_), channel_id=1, source_target_pairs={{0,1},{1,0},{2,3},{3,2},{4,5},{5,4},{6,7},{7,6}} | collective-permute-start | bytes 2555912 | tf_op jit(solution)/shard_map/ppermute | solution.py:278
  324.9 5.3 %collective-permute-start.33 = (bf16[416,1024]{1,0:T(8,128)(2,1)S(1)}, bf16[416,1024]{1,0:T(8,128)(2,1)S(1)}, u32[]{:S(2)}, u32[]{:S(2)}) collective-permute-start(bf16[416,1024]{1,0:T(8,128)(2,1)S(1)} %collective-permute-done.29.refs_2_), channel_id=1, source_target_pairs={{0,1},{1,0},{2,3},{3,2},{4,5},{5,4},{6,7},{7,6}} | collective-permute-start | bytes 2555912 | tf_op jit(solution)/shard_map/ppermute | solution.py:278
  325.9 21.4 %collective-permute-start.23 = (bf16[128,3328]{1,0:T(8,128)(2,1)S(1)}, bf16[128,3328]{1,0:T(8,128)(2,1)S(1)}, u32[]{:S(2)}, u32[]{:S(2)}) collective-permute-start(bf16[128,3328]{1,0:T(8,128)(2,1)S(1)} %collective-permute-done.21.refs_1_), channel_id=1, source_target_pairs={{0,2},{1,3},{2,0},{3,1},{4,6},{5,7},{6,4},{7,5}} | collective-permute-start | bytes 2555912 | tf_op jit(solution)/shard_map/ppermute | solution.py:278
  327.3 20.8 %collective-permute-start.25 = (bf16[128,3328]{1,0:T(8,128)(2,1)S(1)}, bf16[128,3328]{1,0:T(8,128)(2,1)S(1)}, u32[]{:S(2)}, u32[]{:S(2)}) collective-permute-start(bf16[128,3328]{1,0:T(8,128)(2,1)S(1)} %collective-permute-done.21.refs_1_), channel_id=1, source_target_pairs={{0,1},{1,0},{2,3},{3,2},{4,5},{5,4},{6,7},{7,6}} | collective-permute-start | bytes 2555912 | tf_op jit(solution)/shard_map/ppermute | solution.py:278
  327.6 22.0 %collective-permute-start.26 = (bf16[128,3328]{1,0:T(8,128)(2,1)S(1)}, bf16[128,3328]{1,0:T(8,128)(2,1)S(1)}, u32[]{:S(2)}, u32[]{:S(2)}) collective-permute-start(bf16[128,3328]{1,0:T(8,128)(2,1)S(1)} %collective-permute-done.22.refs_2_), channel_id=1, source_target_pairs={{0,1},{1,0},{2,3},{3,2},{4,5},{5,4},{6,7},{7,6}} | collective-permute-start | bytes 2555912 | tf_op jit(solution)/shard_map/ppermute | solution.py:278
  329.6 22.0 %collective-permute-start.16 = (bf16[128,3328]{1,0:T(8,128)(2,1)S(1)}, bf16[128,3328]{1,0:T(8,128)(2,1)}, u32[]{:S(2)}, u32[]{:S(2)}) collective-permute-start(bf16[128,3328]{1,0:T(8,128)(2,1)S(1)} %collective-permute-done.14.refs_1_), channel_id=1, source_target_pairs={{0,4},{1,5},{2,6},{3,7},{4,0},{5,1},{6,2},{7,3}} | collective-permute-start | bytes 2555912 | tf_op jit(solution)/shard_map/ppermute | solution.py:278
  331.1 21.8 %collective-permute-start.18 = (bf16[128,3328]{1,0:T(8,128)(2,1)S(1)}, bf16[128,3328]{1,0:T(8,128)(2,1)S(1)}, u32[]{:S(2)}, u32[]{:S(2)}) collective-permute-start(bf16[128,3328]{1,0:T(8,128)(2,1)S(1)} %collective-permute-done.14.refs_1_), channel_id=1, source_target_pairs={{0,1},{1,0},{2,3},{3,2},{4,5},{5,4},{6,7},{7,6}} | collective-permute-start | bytes 2555912 | tf_op jit(solution)/shard_map/ppermute | solution.py:278
  347.2 7.1 %collective-permute-start.19 = (bf16[128,3328]{1,0:T(8,128)(2,1)S(1)}, bf16[128,3328]{1,0:T(8,128)(2,1)S(1)}, u32[]{:S(2)}, u32[]{:S(2)}) collective-permute-start(bf16[128,3328]{1,0:T(8,128)(2,1)S(1)} %collective-permute-done.15.refs_2_), channel_id=1, source_target_pairs={{0,1},{1,0},{2,3},{3,2},{4,5},{5,4},{6,7},{7,6}} | collective-permute-start | bytes 2555912 | tf_op jit(solution)/shard_map/ppermute | solution.py:278
  349.0 21.4 %collective-permute-start.9 = (bf16[128,3328]{1,0:T(8,128)(2,1)S(1)}, bf16[128,3328]{1,0:T(8,128)(2,1)S(1)}, u32[]{:S(2)}, u32[]{:S(2)}) collective-permute-start(bf16[128,3328]{1,0:T(8,128)(2,1)S(1)} %collective-permute-done.7.refs_1_), channel_id=1, source_target_pairs={{0,2},{1,3},{2,0},{3,1},{4,6},{5,7},{6,4},{7,5}} | collective-permute-start | bytes 2555912 | tf_op jit(solution)/shard_map/ppermute | solution.py:278
  350.5 20.9 %collective-permute-start.11 = (bf16[128,3328]{1,0:T(8,128)(2,1)S(1)}, bf16[128,3328]{1,0:T(8,128)(2,1)S(1)}, u32[]{:S(2)}, u32[]{:S(2)}) collective-permute-start(bf16[128,3328]{1,0:T(8,128)(2,1)S(1)} %collective-permute-done.7.refs_1_), channel_id=1, source_target_pairs={{0,1},{1,0},{2,3},{3,2},{4,5},{5,4},{6,7},{7,6}} | collective-permute-start | bytes 2555912 | tf_op jit(solution)/shard_map/ppermute | solution.py:278
  351.6 22.1 %collective-permute-start.12 = (bf16[128,3328]{1,0:T(8,128)(2,1)S(1)}, bf16[128,3328]{1,0:T(8,128)(2,1)S(1)}, u32[]{:S(2)}, u32[]{:S(2)}) collective-permute-start(bf16[128,3328]{1,0:T(8,128)(2,1)S(1)} %collective-permute-done.8.refs_2_), channel_id=1, source_target_pairs={{0,1},{1,0},{2,3},{3,2},{4,5},{5,4},{6,7},{7,6}} | collective-permute-start | bytes 2555912 | tf_op jit(solution)/shard_map/ppermute | solution.py:278
  353.8 21.8 %collective-permute-start.2 = (bf16[128,3328]{1,0:T(8,128)(2,1)}, bf16[128,3328]{1,0:T(8,128)(2,1)}, u32[]{:S(2)}, u32[]{:S(2)}) collective-permute-start(bf16[128,3328]{1,0:T(8,128)(2,1)} %collective-permute-done.refs_1_), channel_id=1, source_target_pairs={{0,4},{1,5},{2,6},{3,7},{4,0},{5,1},{6,2},{7,3}} | collective-permute-start | bytes 2555912 | tf_op jit(solution)/shard_map/ppermute | solution.py:278
  355.2 20.8 %collective-permute-start.41 = (bf16[416,1024]{1,0:T(8,128)(2,1)S(1)}, bf16[416,1024]{1,0:T(8,128)(2,1)S(1)}, u32[]{:S(2)}, u32[]{:S(2)}) collective-permute-start(bf16[416,1024]{1,0:T(8,128)(2,1)S(1)} %collective-permute-done.37.refs_3_), channel_id=1, source_target_pairs={{0,1},{1,0},{2,3},{3,2},{4,5},{5,4},{6,7},{7,6}} | collective-permute-start | bytes 2555912 | tf_op jit(solution)/shard_map/ppermute | solution.py:278
  370.4 6.6 %collective-permute-start.34 = (bf16[416,1024]{1,0:T(8,128)(2,1)S(1)}, bf16[416,1024]{1,0:T(8,128)(2,1)S(1)}, u32[]{:S(2)}, u32[]{:S(2)}) collective-permute-start(bf16[416,1024]{1,0:T(8,128)(2,1)S(1)} %collective-permute-done.30.refs_3_), channel_id=1, source_target_pairs={{0,1},{1,0},{2,3},{3,2},{4,5},{5,4},{6,7},{7,6}} | collective-permute-start | bytes 2555912 | tf_op jit(solution)/shard_map/ppermute | solution.py:278
  372.3 6.1 %collective-permute-start.27 = (bf16[128,3328]{1,0:T(8,128)(2,1)S(1)}, bf16[128,3328]{1,0:T(8,128)(2,1)S(1)}, u32[]{:S(2)}, u32[]{:S(2)}) collective-permute-start(bf16[128,3328]{1,0:T(8,128)(2,1)S(1)} %collective-permute-done.23.refs_3_), channel_id=1, source_target_pairs={{0,1},{1,0},{2,3},{3,2},{4,5},{5,4},{6,7},{7,6}} | collective-permute-start | bytes 2555912 | tf_op jit(solution)/shard_map/ppermute | solution.py:278
  374.6 4.7 %collective-permute-start.13 = (bf16[128,3328]{1,0:T(8,128)(2,1)S(1)}, bf16[128,3328]{1,0:T(8,128)(2,1)S(1)}, u32[]{:S(2)}, u32[]{:S(2)}) collective-permute-start(bf16[128,3328]{1,0:T(8,128)(2,1)S(1)} %collective-permute-done.9.refs_3_), channel_id=1, source_target_pairs={{0,1},{1,0},{2,3},{3,2},{4,5},{5,4},{6,7},{7,6}} | collective-permute-start | bytes 2555912 | tf_op jit(solution)/shard_map/ppermute | solution.py:278
  375.6 33.3 %collective-permute-start.20 = (bf16[128,3328]{1,0:T(8,128)(2,1)}, bf16[128,3328]{1,0:T(8,128)(2,1)}, u32[]{:S(2)}, u32[]{:S(2)}) collective-permute-start(bf16[128,3328]{1,0:T(8,128)(2,1)} %collective-permute-done.16.refs_3_), channel_id=1, source_target_pairs={{0,1},{1,0},{2,3},{3,2},{4,5},{5,4},{6,7},{7,6}} | collective-permute-start | bytes 2555912 | tf_op jit(solution)/shard_map/ppermute | solution.py:278
  377.0 36.3 %collective-permute-start.3 = (bf16[128,3328]{1,0:T(8,128)(2,1)}, bf16[128,3328]{1,0:T(8,128)(2,1)}, u32[]{:S(2)}, u32[]{:S(2)}) collective-permute-start(bf16[128,3328]{1,0:T(8,128)(2,1)} %get-tuple-element.27.refs_0_), channel_id=1, source_target_pairs={{0,1},{1,0},{2,3},{3,2},{4,5},{5,4},{6,7},{7,6}} | collective-permute-start | bytes 2555912 | tf_op jit(solution)/shard_map/ppermute | solution.py:278
  377.9 35.4 %collective-permute-start.4 = (bf16[128,3328]{1,0:T(8,128)(2,1)}, bf16[128,3328]{1,0:T(8,128)(2,1)}, u32[]{:S(2)}, u32[]{:S(2)}) collective-permute-start(bf16[128,3328]{1,0:T(8,128)(2,1)} %collective-permute-done.refs_1_), channel_id=1, source_target_pairs={{0,1},{1,0},{2,3},{3,2},{4,5},{5,4},{6,7},{7,6}} | collective-permute-start | bytes 2555912 | tf_op jit(solution)/shard_map/ppermute | solution.py:278
  379.3 34.0 %collective-permute-start.5 = (bf16[128,3328]{1,0:T(8,128)(2,1)}, bf16[128,3328]{1,0:T(8,128)(2,1)}, u32[]{:S(2)}, u32[]{:S(2)}) collective-permute-start(bf16[128,3328]{1,0:T(8,128)(2,1)} %collective-permute-done.1.refs_2_), channel_id=1, source_target_pairs={{0,1},{1,0},{2,3},{3,2},{4,5},{5,4},{6,7},{7,6}} | collective-permute-start | bytes 2555912 | tf_op jit(solution)/shard_map/ppermute | solution.py:278
  380.2 33.1 %collective-permute-start.6 = (bf16[128,3328]{1,0:T(8,128)(2,1)}, bf16[128,3328]{1,0:T(8,128)(2,1)}, u32[]{:S(2)}, u32[]{:S(2)}) collective-permute-start(bf16[128,3328]{1,0:T(8,128)(2,1)} %collective-permute-done.2.refs_3_), channel_id=1, source_target_pairs={{0,1},{1,0},{2,3},{3,2},{4,5},{5,4},{6,7},{7,6}} | collective-permute-start | bytes 2555912 | tf_op jit(solution)/shard_map/ppermute | solution.py:278
  (66 other events, 289.6 us)
